TPU v7x, 8 devices: a whole 2x2x1 slice. The times are simulated.
8 devices in a mesh: rep: 2 (over z, y), rows: 4 (over x, core).
Axes of the slice: x: 2, y: 2, z: 1, core: 2. Of those that a mesh axis runs over, the one named last changes fastest.
Arguments:
- adjacency: bfloat16 [16384, 16384], P('rows', 'rep')
- block_mask: int32 [4, 4], replicated
- features: bfloat16 [16384, 128], P('rows')
- w_one: bfloat16 [128, 256], replicated
- w_two: bfloat16 [256, 172], replicated
Outputs:
- output: float32 [16384, 172], P('rows')
All inputs are finite; a program needn't handle non-finite values.
Results may differ from a plain program's by a relative error of at most 0.001.
Values are sent between devices in bfloat16 or wider.
A program may use at most 1 GiB of HBM per device.

v0:
```python
import jax
import jax.numpy as jnp
from jax import lax
from jax.sharding import PartitionSpec as P


def solution(mesh):
    rep_size = mesh.shape['rep']
    rows_size = mesh.shape['rows']
    stage_count = rows_size // rep_size
    perm_pairs = [(src_rep * rows_size + src_row, (src_row // stage_count) * rows_size + (src_row % stage_count) * rep_size + src_rep) for src_rep in range(rep_size) for src_row in range(rows_size)]

    def range_rows(feat_blk):
        rep_idx = lax.axis_index('rep')
        piece_rows = feat_blk.shape[0] // rep_size
        send_piece = lax.dynamic_slice_in_dim(feat_blk, rep_idx * piece_rows, piece_rows, 0)
        recv_piece = lax.ppermute(send_piece, ('rep', 'rows'), perm_pairs)
        return lax.all_gather(recv_piece, 'rows', axis=0, tiled=True)

    def aggregate(adj_local, block_mask, feat_blk):
        rows_idx = lax.axis_index('rows')
        rep_idx = lax.axis_index('rep')
        gathered = range_rows(feat_blk)
        blk_rows = feat_blk.shape[0]
        feat_width = feat_blk.shape[1]
        mask_part = lax.dynamic_slice(block_mask, (rows_idx, rep_idx * stage_count), (1, stage_count))
        masked = (gathered.reshape(stage_count, blk_rows, feat_width) * mask_part.astype(gathered.dtype).reshape(stage_count, 1, 1)).reshape(stage_count * blk_rows, feat_width)
        part_sum = jnp.dot(adj_local, masked, preferred_element_type=jnp.float32)
        return lax.psum(part_sum, 'rep').astype(jnp.bfloat16)

    def local_fn(adj_local, block_mask, feat_blk, w_one, w_two):
        y_one = aggregate(adj_local, block_mask, feat_blk)
        z_one = jnp.maximum(jnp.dot(y_one, w_one, preferred_element_type=jnp.float32), 0.0).astype(jnp.bfloat16)
        y_two = aggregate(adj_local, block_mask, z_one)
        return jnp.dot(y_two, w_two, preferred_element_type=jnp.float32)

    return jax.shard_map(local_fn, mesh=mesh, in_specs=(P('rows', 'rep'), P(), P('rows', None), P(), P()), out_specs=P('rows', None), check_vma=False)
```

profile of v0, /device:TPU:0, one launch (start us, length us, event | category | flops | bytes accessed | tf_op | source)
XLA Modules:
  0.0 320.0 jit_solution(9409035671116569481)
XLA Ops:
  6.5 0.0 copy-start
  6.5 0.0 all-gather.3.cloned.1.call-start
  6.5 1.2 copy-done
  7.8 0.7 collective-permute-start
  8.5 0.0 collective-permute-done
  8.5 0.0 copy-start.2
  8.5 0.8 copy-done.2
  9.3 0.0 all-gather.3.cloned.1.call-update
  9.3 0.0 all-gather.5.cloned.1.call-start
  9.4 0.8 convert_bitcast_fusion
  10.2 0.1 broadcast_bitcast_fusion
  10.2 32.0 %all-gather.3.cloned.1.call-done = bf16[8192,128]{1,0:T(8,128)(2,1)} async-done(((bf16[2048,128]{1,0:T(8,128)(2,1)}), bf16[8192,128]{1,0:T(8,128)(2,1)}) %all-gather.3.cloned.1.call-update) | async-done | bytes 2097168 | tf_op jit(solution)/shard_map/all_gather | solution.py:18
  42.2 30.6 %convolution_bitcast_fusion.1 = f32[4096,128]{0,1:T(8,128)S(1)} fusion(bf16[4096,8192]{1,0:T(8,128)(2,1)} %param.5, bf16[8192,128]{1,0:T(8,128)(2,1)} %all-gather.3.cloned.1.call-done, bf16[8192]{0:T(1024)(128)(2,1)S(1)} %bitcast.15), kind=kOutput, calls=%fused_computation.1 | convolution fusion | flops 8590983168 | bytes 71319552 | tf_op jit(solution)/shard_map/dot_general | solution.py:28
  72.8 0.0 copy-start.4
  72.8 53.9 %all-reduce.2 = bf16[4096,128]{0,1:T(8,128)(2,1)} all-reduce(f32[4096,128]{0,1:T(8,128)S(1)} %convolution_bitcast_fusion.1), channel_id=1, replica_groups=mesh['rep'=2,'rows'=4] {'rep'}, use_global_device_ids=true, to_apply=%region_0.0 | all-reduce | flops 524288 | bytes 3145728 | tf_op jit(solution)/shard_map/psum | solution.py:29
  126.8 0.0 copy-done.4
  126.8 2.0 fusion.10
  128.7 0.2 fusion.1
  128.9 0.7 collective-permute-start.1
  129.7 0.0 collective-permute-done.1
  129.7 0.0 copy-start.1
  129.7 1.0 copy-done.1
  130.7 0.0 all-gather.5.cloned.1.call-update
  130.7 47.6 %all-gather.5.cloned.1.call-done = bf16[8192,256]{1,0:T(8,128)(2,1)} async-done(((bf16[2048,256]{1,0:T(8,128)(2,1)}), bf16[8192,256]{1,0:T(8,128)(2,1)}) %all-gather.5.cloned.1.call-update) | async-done | bytes 4194320 | tf_op jit(solution)/shard_map/all_gather | solution.py:18
  178.3 31.2 %convolution_bitcast_fusion = f32[4096,256]{0,1:T(8,128)} fusion(bf16[4096,8192]{1,0:T(8,128)(2,1)} %param.5, bf16[8192,256]{1,0:T(8,128)(2,1)} %all-gather.5.cloned.1.call-done, bf16[8192]{0:T(1024)(128)(2,1)S(1)} %bitcast.16), kind=kOutput, calls=%fused_computation | convolution fusion | flops 17181966336 | bytes 75513856 | tf_op jit(solution)/shard_map/dot_general | solution.py:28
  209.5 0.0 copy-start.3
  209.5 101.5 %all-reduce.3 = bf16[4096,256]{0,1:T(8,128)(2,1)S(1)} all-reduce(f32[4096,256]{0,1:T(8,128)} %convolution_bitcast_fusion), channel_id=1, replica_groups=mesh['rep'=2,'rows'=4] {'rep'}, use_global_device_ids=true, to_apply=%region_1.0 | all-reduce | flops 1048576 | bytes 6291456 | tf_op jit(solution)/shard_map/psum | solution.py:29
  311.1 0.0 copy-done.3
  311.1 2.1 fusion.9
  (2 shorter events, 0.0 us)
Async XLA Ops:
  6.5 1.2 copy-start
  6.5 35.7 %all-gather.3.cloned.1.call-start = ((), (), s32[]{:S(2)}) async-start(), calls=%async_computation | async-start | bytes 2621440 | tf_op jit(solution)/shard_map/all_gather | solution.py:18
  7.8 0.7 collective-permute-start
  8.5 0.8 copy-start.2
  9.3 169.0 %all-gather.5.cloned.1.call-start = ((), (), s32[]{:S(2)}) async-start(), calls=%async_computation.1 | async-start | bytes 5242880 | tf_op jit(solution)/shard_map/all_gather | solution.py:18
  72.8 53.9 %copy-start.4 = (bf16[128,256]{1,0:T(8,128)(2,1)S(1)}, bf16[128,256]{1,0:T(8,128)(2,1)}, u32[]{:S(2)}) copy-start(bf16[128,256]{1,0:T(8,128)(2,1)} %param.8) | copy-start | bytes 196612
  128.9 0.7 collective-permute-start.1
  129.7 1.0 copy-start.1
  209.5 101.5 %copy-start.3 = (bf16[256,172]{0,1:T(8,128)(2,1)S(1)}, bf16[256,172]{0,1:T(8,128)(2,1)}, u32[]{:S(2)}) copy-start(bf16[256,172]{0,1:T(8,128)(2,1)} %param.9) | copy-start | bytes 264196
Sparse Core Ops, SparseCore 0:
  9.5 32.7 all-gather.2
  130.8 47.4 all-gather.4
where the time goes:
time: 320 us
  blocking collectives  155 us (48%)
  waiting for transfers between devices  79.6 us (25%)
  matrix products  65.9 us (21%)
  between operations  13.5 us (4%)
    psum x2, blocking collectives, aggregate(): return lax.psum(part_sum, 'rep').astype(jnp.bfloat16)  155 us
    all_gather x2, waiting for transfers between devices, range_rows(): return lax.all_gather(recv_piece, 'rows', axis=0, tiled=True)  79.6 us
    dot_general x2, matrix products, aggregate(): part_sum = jnp.dot(adj_local, masked, preferred_element_type=jnp.float32)  61.8 us
  transfers between devices with their start and end apart: 4, of which 2 were waited for; matrix products, arithmetic and copies ran while one was open for 0% of the time, Pallas kernels for 0%

commit v1 on v0

v1 whole, which is shorter than its diff:
```python
import jax
import jax.numpy as jnp
from jax import lax
from jax.experimental import pallas as pl
from jax.experimental.pallas import tpu as pltpu
from jax.sharding import PartitionSpec as P

MESH = pl.DeviceIdType.MESH
BLK = 4096
CH = 256
NCH = BLK // CH
HALF = NCH // 2
NBUF = 3
F0 = 128
F1 = 256
F32 = jnp.float32
BF16 = jnp.bfloat16


def loop(lo, hi, fn):
    def body(idx, carry):
        fn(idx)
        return carry
    lax.fori_loop(lo, hi, body, 0)


def kernel(mask_ref, w1_ref, a_ref, h_ref, y2_ref,
           abuf_r, abuf_c, hbuf, ht, w1t, pbuf_s, pbuf_r, mbuf_s, mbuf_r, own1, ybuf, ybuf_i, z, zt,
           dfb, tms, tmr, own2, tfb, y2s,
           ar_sem, ac_sem, h_sem, hx_s, hx_r, pf_s, pf_r, mf_s, mf_r, pb_s, pb_r, mb_s, mb_r, yb_s, yb_r,
           df_s, df_r, tm_s, tm_r, tf_s, tf_r, ob_s, ob_r, out_sem):
    rep = lax.axis_index('rep')
    row = lax.axis_index('rows')
    chip_x = row // 2
    core = row % 2
    diag = chip_x == rep
    other = 1 - core
    partner = (rep, (1 - chip_x) * 2 + core)
    mate = (rep, chip_x * 2 + other)
    yside = (1 - rep, row)
    blk_own = rep * 2 + core
    blk_other = rep * 2 + other

    def remote(src, dst, send, recv, dev):
        return pltpu.make_async_remote_copy(src_ref=src, dst_ref=dst, send_sem=send, recv_sem=recv, device_id=dev, device_id_type=MESH)

    def row_copy(m, slot):
        return pltpu.make_async_copy(a_ref.at[pl.ds(pl.multiple_of(m * CH, CH), CH), :], abuf_r.at[slot], ar_sem.at[slot])

    def col_copy(q, slot, k):
        return pltpu.make_async_copy(a_ref.at[:, pl.ds(pl.multiple_of(k * BLK + q * CH, CH), CH)], abuf_c.at[slot, k], ac_sem.at[slot, k])

    def h_send():
        return remote(h_ref, hbuf.at[core], hx_s, hx_r, mate)

    def pf(r):
        return remote(pbuf_s.at[r], pbuf_r.at[r], pf_s.at[r], pf_r.at[r], partner)

    def mf(m):
        return remote(mbuf_s.at[m], mbuf_r.at[m], mf_s.at[m], mf_r.at[m], mate)

    def pb(m, r):
        return remote(ybuf.at[core, m], ybuf.at[core, m], pb_s.at[r], pb_r.at[r], partner)

    def mb_out(m):
        return remote(ybuf.at[core, m], ybuf.at[core, m], mb_s.at[m], mb_r.at[m], mate)

    def mb_in(m):
        return remote(ybuf.at[other, m], ybuf.at[other, m], mb_s.at[m], mb_r.at[m], mate)

    def yb(m):
        return remote(ybuf.at[core, m], ybuf_i.at[m], yb_s.at[m], yb_r.at[m], yside)

    def df(m):
        return remote(dfb.at[m], dfb.at[m], df_s.at[m], df_r.at[m], yside)

    def tm(m):
        return remote(tms.at[m], tmr.at[m], tm_s.at[m], tm_r.at[m], mate)

    def tf(m):
        return remote(tfb.at[m], tfb.at[m], tf_s.at[m], tf_r.at[m], partner)

    def out_rows(m):
        return y2_ref.at[pl.ds(pl.multiple_of(m * CH, CH), CH), :]

    def ob(m):
        return remote(y2s.at[m], out_rows(m), ob_s.at[m], ob_r.at[m], yside)

    def out_copy(m):
        return pltpu.make_async_copy(y2s.at[m], out_rows(m), out_sem.at[m])

    def mask_of(dst_blk, src_blk):
        return mask_ref[dst_blk, src_blk].astype(F32)

    def hidden_rows(k, m):
        hid = jnp.maximum(jnp.dot(ybuf[k, m], w1_ref[...], preferred_element_type=F32), 0.0)
        z[pl.ds(pl.multiple_of(k * BLK + m * CH, CH), CH), :] = (hid * mask_of(row, rep * 2 + k)).astype(BF16)

    def barrier():
        sem = pltpu.get_barrier_semaphore()
        for dev in (partner, mate, yside):
            pl.semaphore_signal(sem, inc=1, device_id=dev, device_id_type=MESH)
        pl.semaphore_wait(sem, 3)

    h_own = pltpu.make_async_copy(h_ref, hbuf.at[core], h_sem)
    h_own.start()

    @pl.when(diag)
    def _():
        for t in range(NBUF):
            row_copy(t + HALF, t).start()

    @pl.when(jnp.logical_not(diag))
    def _():
        for t in range(NBUF):
            for k in range(2):
                col_copy(t, t, k).start()

    barrier()

    @pl.when(diag)
    def _():
        h_send().start()

        def chunk_at(t):
            first = (t + HALF) % NCH
            second = t - NCH
            return jnp.where(t < NCH, first, second // 2 + HALF * (second % 2))

        def next_load(t):
            nxt = t + NBUF

            @pl.when(nxt < 2 * NCH)
            def _():
                row_copy(chunk_at(nxt), nxt % NBUF).start()

        h_own.wait()
        hbuf[core] = (hbuf[core].astype(F32) * mask_of(row, blk_own)).astype(BF16)
        remote(h_ref, hbuf.at[other], hx_s, hx_r, mate).wait_recv()
        hbuf[other] = (hbuf[other].astype(F32) * mask_of(row, blk_other)).astype(BF16)

        def product1(t):
            slot = t % NBUF
            row_copy(0, slot).wait()
            return jnp.dot(abuf_r[slot], hbuf[...].reshape(2 * BLK, F0), preferred_element_type=F32)

        def send_half(t):
            pbuf_s[t] = product1(t)
            pf(t).start()
            next_load(t)
        loop(0, HALF, send_half)

        def keep_half(r):
            t = r + HALF
            part = product1(t)
            next_load(t)
            pf(r).wait_recv()
            ybuf[core, r] = (part + pbuf_r[r]).astype(BF16)
            pb(r, r).start()
            yb(r).start()
            mb_out(r).start()
            hidden_rows(core, r)
        loop(0, HALF, keep_half)

        def relay(r):
            m = r + HALF
            pb(m, r).wait_recv()
            yb(m).start()
            mb_out(m).start()
            hidden_rows(core, m)
            mb_in(r).wait_recv()
            hidden_rows(other, r)
        loop(0, HALF, relay)

        def rest(r):
            mb_in(r + HALF).wait_recv()
            hidden_rows(other, r + HALF)
        loop(0, HALF, rest)

        def layer2(s):
            t = s + NCH
            slot = t % NBUF
            m = chunk_at(t)
            row_copy(0, slot).wait()
            part = jnp.dot(abuf_r[slot], z[...], preferred_element_type=F32)
            next_load(t)
            half = s // 2

            def finish(got):
                y2s[m] = (part + got).astype(BF16)

            @pl.when(s % 2 == 0)
            def _():
                df(half).wait_recv()
                finish(dfb[half])

            @pl.when(s % 2 == 1)
            def _():
                tf(half).wait_recv()
                finish(tfb[half])
            ob(m).start()
            out_copy(m).start()
        loop(0, NCH, layer2)

        h_send().wait_send()

        def drain_half(r):
            pf(r).wait_send()
            pb(r, r).wait_send()
        loop(0, HALF, drain_half)

        def drain(m):
            yb(m).wait_send()
            mb_out(m).wait_send()
            ob(m).wait_send()
            out_copy(m).wait()
        loop(0, NCH, drain)

    @pl.when(jnp.logical_not(diag))
    def _():
        def next_cols(t):
            nxt = t + NBUF

            @pl.when(nxt < NCH + HALF)
            def _():
                q = jnp.where(nxt < NCH, nxt, nxt - HALF)
                for k in range(2):
                    col_copy(q, nxt % NBUF, k).start()

        def cols_wait(slot):
            for k in range(2):
                col_copy(0, slot, k).wait()

        w1t[...] = w1_ref[...].astype(F32).T.astype(BF16)
        h_own.wait()

        def turn(m):
            piece = hbuf[core, pl.ds(pl.multiple_of(m * CH, CH), CH), :]
            ht[:, pl.ds(pl.multiple_of(m * CH, CH), CH)] = piece.astype(F32).T.astype(BF16)
        loop(0, NCH, turn)

        mask_own = mask_of(blk_own, row)
        mask_other = mask_of(blk_other, row)

        def produce1(t):
            slot = t % NBUF
            cols_wait(slot)
            mbuf_s[t] = jnp.dot(ht[...], abuf_c[slot, other], preferred_element_type=F32) * mask_other
            mf(t).start()
            own1[t % 2] = jnp.dot(ht[...], abuf_c[slot, core], preferred_element_type=F32) * mask_own
            next_cols(t)

        def combine1(t):
            mf(t).wait_recv()
            return (own1[t % 2] + mbuf_r[t]).T

        def combine_send(t):
            pbuf_s[t] = combine1(t)
            pf(t).start()

        def combine_keep(r):
            m = r + HALF
            part = combine1(m)
            pf(r).wait_recv()
            ybuf[core, m] = (part + pbuf_r[r]).astype(BF16)
            pb(m, r).start()
            mb_out(m).start()
            hidden_rows(core, m)

        produce1(0)

        def send_half(t):
            produce1(t + 1)
            combine_send(t)
        loop(0, HALF, send_half)

        def keep_half(r):
            produce1(r + HALF + 1)
            combine_keep(r)
        loop(0, HALF - 1, keep_half)
        combine_keep(HALF - 1)

        for v in range(NBUF):
            row_copy(v, v).start()

        def hidden_turned(m):
            yb(m).wait_recv()
            hid = lax.dot_general(w1t[...], ybuf_i[m], (((1,), (1,)), ((), ())), preferred_element_type=F32)
            zt[:, pl.ds(pl.multiple_of(m * CH, CH), CH)] = jnp.maximum(hid, 0.0).astype(BF16)

        def relay(r):
            pb(r, r).wait_recv()
            mb_out(r).start()
            hidden_rows(core, r)
            mb_in(r + HALF).wait_recv()
            hidden_rows(other, r + HALF)
            hidden_turned(r)
        loop(0, HALF, relay)

        def rest(r):
            mb_in(r).wait_recv()
            hidden_rows(other, r)
            hidden_turned(r + HALF)
        loop(0, HALF, rest)

        def produce2(m):
            slot_r = m % NBUF
            row_copy(0, slot_r).wait()
            dfb[m] = jnp.dot(abuf_r[slot_r], z[...], preferred_element_type=F32)
            df(m).start()

            @pl.when(m + NBUF < HALF)
            def _():
                row_copy(m + NBUF, slot_r).start()
            t = m + NCH
            slot = t % NBUF
            cols_wait(slot)
            tms[m] = jnp.dot(zt[...], abuf_c[slot, other], preferred_element_type=F32) * mask_other
            tm(m).start()
            own2[m % 2] = jnp.dot(zt[...], abuf_c[slot, core], preferred_element_type=F32) * mask_own
            next_cols(t)

        def combine2(m):
            tm(m).wait_recv()
            tfb[m] = (own2[m % 2] + tmr[m]).T
            tf(m).start()

        produce2(0)

        def layer2(m):
            produce2(m + 1)
            combine2(m)
        loop(0, HALF - 1, layer2)
        combine2(HALF - 1)

        def receive(m):
            ob(m).wait_recv()
        loop(0, NCH, receive)

        def drain_half(r):
            pf(r).wait_send()
            pb(r + HALF, r).wait_send()
            df(r).wait_send()
            tm(r).wait_send()
            tf(r).wait_send()
        loop(0, HALF, drain_half)

        def drain(m):
            mf(m).wait_send()
            mb_out(m).wait_send()
        loop(0, NCH, drain)


def solution(mesh):
    def local_fn(adj_local, block_mask, feat_blk, w_one, w_two):
        dma = pltpu.SemaphoreType.DMA
        y_two = pl.pallas_call(
            kernel,
            out_shape=jax.ShapeDtypeStruct((BLK, F1), BF16),
            in_specs=[pl.BlockSpec(memory_space=pltpu.SMEM), pl.BlockSpec(memory_space=pltpu.VMEM), pl.BlockSpec(memory_space=pl.ANY), pl.BlockSpec(memory_space=pl.ANY)],
            out_specs=pl.BlockSpec(memory_space=pl.ANY),
            scratch_shapes=[
                pltpu.VMEM((NBUF, CH, 2 * BLK), BF16),
                pltpu.VMEM((NBUF, 2, BLK, CH), BF16),
                pltpu.VMEM((2, BLK, F0), BF16),
                pltpu.VMEM((F0, BLK), BF16),
                pltpu.VMEM((F1, F0), BF16),
                pltpu.VMEM((HALF, CH, F0), F32),
                pltpu.VMEM((HALF, CH, F0), F32),
                pltpu.VMEM((NCH, F0, CH), F32),
                pltpu.VMEM((NCH, F0, CH), F32),
                pltpu.VMEM((2, F0, CH), F32),
                pltpu.VMEM((2, NCH, CH, F0), BF16),
                pltpu.VMEM((NCH, CH, F0), BF16),
                pltpu.VMEM((2 * BLK, F1), BF16),
                pltpu.VMEM((F1, BLK), BF16),
                pltpu.VMEM((HALF, CH, F1), F32),
                pltpu.VMEM((HALF, F1, CH), F32),
                pltpu.VMEM((HALF, F1, CH), F32),
                pltpu.VMEM((2, F1, CH), F32),
                pltpu.VMEM((HALF, CH, F1), F32),
                pltpu.VMEM((NCH, CH, F1), BF16),
                dma((NBUF,)), dma((NBUF, 2)), dma, dma, dma,
                dma((HALF,)), dma((HALF,)), dma((NCH,)), dma((NCH,)), dma((HALF,)), dma((HALF,)),
                dma((NCH,)), dma((NCH,)), dma((NCH,)), dma((NCH,)),
                dma((HALF,)), dma((HALF,)), dma((HALF,)), dma((HALF,)), dma((HALF,)), dma((HALF,)),
                dma((NCH,)), dma((NCH,)), dma((NCH,)),
            ],
            compiler_params=pltpu.CompilerParams(collective_id=0, has_side_effects=True, vmem_limit_bytes=66 * 1000 * 1000),
        )(block_mask, w_one, adj_local, feat_blk)
        return jnp.dot(y_two, w_two, preferred_element_type=F32)

    return jax.shard_map(local_fn, mesh=mesh, in_specs=(P('rows', 'rep'), P(), P('rows', None), P(), P()), out_specs=P('rows', None), check_vma=False)
```

time: 320 us -> 116 us (0.36)
  blocking collectives: 155 us -> 0 us
  Pallas kernels: 0 us -> 112 us
  waiting for transfers between devices: 79.6 us -> 0 us
  matrix products: 65.9 us -> 4.01 us
  between operations: 13.5 us -> 0.02 us
    psum x2 -> x0, blocking collectives: 155 us -> none  [aggregate(): return lax.psum(part_sum, 'rep').astype(jnp.bfloat16)]
    pallas_call x0 -> x1, Pallas kernels: none -> 112 us  [local_fn(): pl.pallas_call(kernel, out_shape=jax.ShapeDtypeStruct((BLK, F1), BF16), i...]
    all_gather x2 -> x0, waiting for transfers between devices: 79.6 us -> none  [range_rows(): return lax.all_gather(recv_piece, 'rows', axis=0, tiled=True)]
    dot_general x4 -> x1, matrix products: 65.9 us -> 4.01 us  [local_fn(): return jnp.dot(y_two, w_two, preferred_element_type=F32)]
  transfers between devices with their start and end apart: 4 -> 0, of which waited for: 2 -> 0; matrix products, arithmetic and copies ran while one was open for 0% -> 0% of each run, Pallas kernels for 0% -> 0%
where the time goes in v1:
time: 116 us
  Pallas kernels  112 us (97%)
  matrix products  4.01 us (3%)
    pallas_call x1, Pallas kernels, local_fn(): pl.pallas_call(kernel, out_shape=jax.ShapeDtypeStruct((BLK, F1), BF16), i...  112 us
    dot_general x1, matrix products, local_fn(): return jnp.dot(y_two, w_two, preferred_element_type=F32)  4.01 us

profile of v1, /device:TPU:0, one launch (start us, length us, event | category | flops | bytes accessed | tf_op | source)
XLA Modules:
  0.0 115.7 jit_solution(12944113940289375808)
XLA Ops:
  0.0 0.0 copy-start
  0.0 111.6 %shard_map.55 = bf16[4096,256]{1,0:T(8,128)(2,1)} custom-call(s32[4,4]{1,0:T(4,128)} %mask_ref.1, bf16[128,256]{1,0:T(8,128)(2,1)} %w1_ref.1, bf16[4096,8192]{1,0:T(8,128)(2,1)} %a_ref.1, bf16[4096,128]{1,0:T(8,128)(2,1)} %h_ref.1), custom_call_target="tpu_custom_call" | custom-call | tf_op jit(solution)/shard_map/pallas_call | solution.py:357
  111.6 0.0 copy-done
  111.6 4.0 %fusion = f32[4096,172]{0,1:T(8,128)} fusion(bf16[4096,256]{1,0:T(8,128)(2,1)} %shard_map.55, bf16[256,172]{0,1:T(8,128)(2,1)S(1)} %copy-done), kind=kOutput, calls=%fused_computation | convolution fusion | flops 360710144 | bytes 5003264 | tf_op jit(solution)/shard_map/dot_general | solution.py:391
Async XLA Ops:
  0.0 111.6 %copy-start = (bf16[256,172]{0,1:T(8,128)(2,1)S(1)}, bf16[256,172]{0,1:T(8,128)(2,1)}, u32[]{:S(2)}) copy-start(bf16[256,172]{0,1:T(8,128)(2,1)} %param.9) | copy-start | bytes 264196

commit v2 on v1

--- a/solution.py
+++ b/solution.py
@@ -11,6 +11,8 @@
 NCH = BLK // CH
 HALF = NCH // 2
 NBUF = 3
+PC = 128
+NPC = CH // PC
 F0 = 128
 F1 = 256
 F32 = jnp.float32
@@ -26,7 +28,7 @@
 
 def kernel(mask_ref, w1_ref, a_ref, h_ref, y2_ref,
            abuf_r, abuf_c, hbuf, ht, w1t, pbuf_s, pbuf_r, mbuf_s, mbuf_r, own1, ybuf, ybuf_i, z, zt,
-           dfb, tms, tmr, own2, tfb, y2s,
+           dfb, tms, tmr, acc2, tfb, y2s,
            ar_sem, ac_sem, h_sem, hx_s, hx_r, pf_s, pf_r, mf_s, mf_r, pb_s, pb_r, mb_s, mb_r, yb_s, yb_r,
            df_s, df_r, tm_s, tm_r, tf_s, tf_r, ob_s, ob_r, out_sem):
     rep = lax.axis_index('rep')
@@ -71,23 +73,25 @@
     def yb(m):
         return remote(ybuf.at[core, m], ybuf_i.at[m], yb_s.at[m], yb_r.at[m], yside)
 
-    def df(m):
-        return remote(dfb.at[m], dfb.at[m], df_s.at[m], df_r.at[m], yside)
+    def df(m, p):
+        part = dfb.at[m, pl.ds(p * PC, PC), :]
+        return remote(part, part, df_s.at[m, p], df_r.at[m, p], yside)
 
     def tm(m):
         return remote(tms.at[m], tmr.at[m], tm_s.at[m], tm_r.at[m], mate)
 
-    def tf(m):
-        return remote(tfb.at[m], tfb.at[m], tf_s.at[m], tf_r.at[m], partner)
-
-    def out_rows(m):
-        return y2_ref.at[pl.ds(pl.multiple_of(m * CH, CH), CH), :]
-
-    def ob(m):
-        return remote(y2s.at[m], out_rows(m), ob_s.at[m], ob_r.at[m], yside)
-
-    def out_copy(m):
-        return pltpu.make_async_copy(y2s.at[m], out_rows(m), out_sem.at[m])
+    def tf(m, p):
+        part = tfb.at[m, pl.ds(p * PC, PC), :]
+        return remote(part, part, tf_s.at[m, p], tf_r.at[m, p], partner)
+
+    def out_rows(m, p):
+        return y2_ref.at[pl.ds(pl.multiple_of(m * CH + p * PC, PC), PC), :]
+
+    def ob(m, p):
+        return remote(y2s.at[m, pl.ds(p * PC, PC), :], out_rows(m, p), ob_s.at[m, p], ob_r.at[m, p], yside)
+
+    def out_copy(m, p):
+        return pltpu.make_async_copy(y2s.at[m, pl.ds(p * PC, PC), :], out_rows(m, p), out_sem.at[m, p])
 
     def mask_of(dst_blk, src_blk):
         return mask_ref[dst_blk, src_blk].astype(F32)
@@ -105,17 +109,19 @@
     h_own = pltpu.make_async_copy(h_ref, hbuf.at[core], h_sem)
     h_own.start()
 
-    @pl.when(diag)
-    def _():
-        for t in range(NBUF):
-            row_copy(t + HALF, t).start()
-
-    @pl.when(jnp.logical_not(diag))
-    def _():
-        for t in range(NBUF):
-            for k in range(2):
-                col_copy(t, t, k).start()
-
+    def first_loads(lo, hi):
+        @pl.when(diag)
+        def _():
+            for t in range(lo, hi):
+                row_copy(t + HALF, t).start()
+
+        @pl.when(jnp.logical_not(diag))
+        def _():
+            for t in range(lo, hi):
+                for k in range(2):
+                    col_copy(t, t, k).start()
+
+    first_loads(0, 1)
     barrier()
 
     @pl.when(diag)
@@ -135,20 +141,29 @@
                 row_copy(chunk_at(nxt), nxt % NBUF).start()
 
         h_own.wait()
-        hbuf[core] = (hbuf[core].astype(F32) * mask_of(row, blk_own)).astype(BF16)
-        remote(h_ref, hbuf.at[other], hx_s, hx_r, mate).wait_recv()
-        hbuf[other] = (hbuf[other].astype(F32) * mask_of(row, blk_other)).astype(BF16)
+        first_loads(1, NBUF)
+
+        def product1_of(slot, k, dst):
+            cols = pl.ds(pl.multiple_of(k * BLK, BLK), BLK)
+            return jnp.dot(abuf_r[slot, :, cols], hbuf[k], preferred_element_type=F32) * mask_of(dst, rep * 2 + k)
 
         def product1(t):
             slot = t % NBUF
             row_copy(0, slot).wait()
-            return jnp.dot(abuf_r[slot], hbuf[...].reshape(2 * BLK, F0), preferred_element_type=F32)
+            return product1_of(slot, 0, row) + product1_of(slot, 1, row)
+
+        row_copy(0, 0).wait()
+        pbuf_s[0] = product1_of(0, core, row)
+        remote(h_ref, hbuf.at[other], hx_s, hx_r, mate).wait_recv()
+        pbuf_s[0] = pbuf_s[0] + product1_of(0, other, row)
+        pf(0).start()
+        next_load(0)
 
         def send_half(t):
             pbuf_s[t] = product1(t)
             pf(t).start()
             next_load(t)
-        loop(0, HALF, send_half)
+        loop(1, HALF, send_half)
 
         def keep_half(r):
             t = r + HALF
@@ -177,30 +192,38 @@
             hidden_rows(other, r + HALF)
         loop(0, HALF, rest)
 
-        def layer2(s):
+        def product2(s):
             t = s + NCH
             slot = t % NBUF
-            m = chunk_at(t)
             row_copy(0, slot).wait()
-            part = jnp.dot(abuf_r[slot], z[...], preferred_element_type=F32)
+            acc2[s % 2] = jnp.dot(abuf_r[slot], z[...], preferred_element_type=F32)
             next_load(t)
+
+        def finish(s):
+            m = chunk_at(s + NCH)
             half = s // 2
-
-            def finish(got):
-                y2s[m] = (part + got).astype(BF16)
-
-            @pl.when(s % 2 == 0)
-            def _():
-                df(half).wait_recv()
-                finish(dfb[half])
-
-            @pl.when(s % 2 == 1)
-            def _():
-                tf(half).wait_recv()
-                finish(tfb[half])
-            ob(m).start()
-            out_copy(m).start()
-        loop(0, NCH, layer2)
+            for p in range(NPC):
+                rows = pl.ds(p * PC, PC)
+
+                @pl.when(s % 2 == 0)
+                def _():
+                    df(half, p).wait_recv()
+                    y2s[m, rows, :] = (acc2[s % 2, rows, :] + dfb[half, rows, :]).astype(BF16)
+
+                @pl.when(s % 2 == 1)
+                def _():
+                    tf(half, p).wait_recv()
+                    y2s[m, rows, :] = (acc2[s % 2, rows, :] + tfb[half, rows, :]).astype(BF16)
+                ob(m, p).start()
+                out_copy(m, p).start()
+
+        product2(0)
+
+        def layer2(s):
+            product2(s + 1)
+            finish(s)
+        loop(0, NCH - 1, layer2)
+        finish(NCH - 1)
 
         h_send().wait_send()
 
@@ -212,8 +235,9 @@
         def drain(m):
             yb(m).wait_send()
             mb_out(m).wait_send()
-            ob(m).wait_send()
-            out_copy(m).wait()
+            for p in range(NPC):
+                ob(m, p).wait_send()
+                out_copy(m, p).wait()
         loop(0, NCH, drain)
 
     @pl.when(jnp.logical_not(diag))
@@ -231,7 +255,6 @@
             for k in range(2):
                 col_copy(0, slot, k).wait()
 
-        w1t[...] = w1_ref[...].astype(F32).T.astype(BF16)
         h_own.wait()
 
         def turn(m):
@@ -242,12 +265,14 @@
         mask_own = mask_of(blk_own, row)
         mask_other = mask_of(blk_other, row)
 
-        def produce1(t):
+        def produce1_other(t):
             slot = t % NBUF
             cols_wait(slot)
             mbuf_s[t] = jnp.dot(ht[...], abuf_c[slot, other], preferred_element_type=F32) * mask_other
             mf(t).start()
-            own1[t % 2] = jnp.dot(ht[...], abuf_c[slot, core], preferred_element_type=F32) * mask_own
+
+        def produce1_own(t):
+            own1[t % 2] = jnp.dot(ht[...], abuf_c[t % NBUF, core], preferred_element_type=F32) * mask_own
             next_cols(t)
 
         def combine1(t):
@@ -267,18 +292,23 @@
             mb_out(m).start()
             hidden_rows(core, m)
 
-        produce1(0)
+        produce1_other(0)
+        first_loads(1, NBUF)
+        produce1_own(0)
 
         def send_half(t):
-            produce1(t + 1)
+            produce1_other(t + 1)
             combine_send(t)
+            produce1_own(t + 1)
         loop(0, HALF, send_half)
 
         def keep_half(r):
-            produce1(r + HALF + 1)
+            produce1_other(r + HALF + 1)
             combine_keep(r)
+            produce1_own(r + HALF + 1)
         loop(0, HALF - 1, keep_half)
         combine_keep(HALF - 1)
+        w1t[...] = w1_ref[...].astype(F32).T.astype(BF16)
 
         for v in range(NBUF):
             row_copy(v, v).start()
@@ -300,49 +330,58 @@
         def rest(r):
             mb_in(r).wait_recv()
             hidden_rows(other, r)
-            hidden_turned(r + HALF)
         loop(0, HALF, rest)
 
-        def produce2(m):
-            slot_r = m % NBUF
-            row_copy(0, slot_r).wait()
-            dfb[m] = jnp.dot(abuf_r[slot_r], z[...], preferred_element_type=F32)
-            df(m).start()
+        def direct(m):
+            slot = m % NBUF
+            row_copy(0, slot).wait()
+            dfb[m] = jnp.dot(abuf_r[slot], z[...], preferred_element_type=F32)
+            for p in range(NPC):
+                df(m, p).start()
 
             @pl.when(m + NBUF < HALF)
             def _():
-                row_copy(m + NBUF, slot_r).start()
-            t = m + NCH
-            slot = t % NBUF
+                row_copy(m + NBUF, slot).start()
+
+        def turned_other(m):
+            slot = (m + NCH) % NBUF
             cols_wait(slot)
             tms[m] = jnp.dot(zt[...], abuf_c[slot, other], preferred_element_type=F32) * mask_other
             tm(m).start()
-            own2[m % 2] = jnp.dot(zt[...], abuf_c[slot, core], preferred_element_type=F32) * mask_own
+
+        def turned_own(m):
+            t = m + NCH
+            own = jnp.dot(zt[...], abuf_c[t % NBUF, core], preferred_element_type=F32) * mask_own
             next_cols(t)
-
-        def combine2(m):
+            acc2[0] = own
             tm(m).wait_recv()
-            tfb[m] = (own2[m % 2] + tmr[m]).T
-            tf(m).start()
-
-        produce2(0)
+            tfb[m] = (acc2[0] + tmr[m]).T
+            for p in range(NPC):
+                tf(m, p).start()
+
+        direct(0)
+        loop(HALF, NCH, hidden_turned)
+        turned_other(0)
+        turned_own(0)
 
         def layer2(m):
-            produce2(m + 1)
-            combine2(m)
-        loop(0, HALF - 1, layer2)
-        combine2(HALF - 1)
+            turned_other(m)
+            direct(m)
+            turned_own(m)
+        loop(1, HALF, layer2)
 
         def receive(m):
-            ob(m).wait_recv()
+            for p in range(NPC):
+                ob(m, p).wait_recv()
         loop(0, NCH, receive)
 
         def drain_half(r):
             pf(r).wait_send()
             pb(r + HALF, r).wait_send()
-            df(r).wait_send()
             tm(r).wait_send()
-            tf(r).wait_send()
+            for p in range(NPC):
+                df(r, p).wait_send()
+                tf(r, p).wait_send()
         loop(0, HALF, drain_half)
 
         def drain(m):
@@ -383,8 +422,8 @@
                 dma((NBUF,)), dma((NBUF, 2)), dma, dma, dma,
                 dma((HALF,)), dma((HALF,)), dma((NCH,)), dma((NCH,)), dma((HALF,)), dma((HALF,)),
                 dma((NCH,)), dma((NCH,)), dma((NCH,)), dma((NCH,)),
-                dma((HALF,)), dma((HALF,)), dma((HALF,)), dma((HALF,)), dma((HALF,)), dma((HALF,)),
-                dma((NCH,)), dma((NCH,)), dma((NCH,)),
+                dma((HALF, NPC)), dma((HALF, NPC)), dma((HALF,)), dma((HALF,)), dma((HALF, NPC)), dma((HALF, NPC)),
+                dma((NCH, NPC)), dma((NCH, NPC)), dma((NCH, NPC)),
             ],
             compiler_params=pltpu.CompilerParams(collective_id=0, has_side_effects=True, vmem_limit_bytes=66 * 1000 * 1000),
         )(block_mask, w_one, adj_local, feat_blk)

time: 116 us -> 109 us (0.940)
  Pallas kernels: 112 us -> 105 us
    pallas_call x1, Pallas kernels: 112 us -> 105 us  [local_fn(): pl.pallas_call(kernel, out_shape=jax.ShapeDtypeStruct((BLK, F1), BF16), i...]
where the time goes in v2:
time: 109 us
  Pallas kernels  105 us (96%)
  matrix products  4.01 us (4%)
    pallas_call x1, Pallas kernels, local_fn(): pl.pallas_call(kernel, out_shape=jax.ShapeDtypeStruct((BLK, F1), BF16), i...  105 us
    dot_general x1, matrix products, local_fn(): return jnp.dot(y_two, w_two, preferred_element_type=F32)  4.01 us

profile of v2, /device:TPU:0, one launch (start us, length us, event | category | flops | bytes accessed | tf_op | source)
XLA Modules:
  0.0 109.0 jit_solution(8653031767683945526)
XLA Ops:
  0.0 0.0 copy-start
  0.0 105.0 %shard_map.55 = bf16[4096,256]{1,0:T(8,128)(2,1)} custom-call(s32[4,4]{1,0:T(4,128)} %mask_ref.1, bf16[128,256]{1,0:T(8,128)(2,1)} %w1_ref.1, bf16[4096,8192]{1,0:T(8,128)(2,1)} %a_ref.1, bf16[4096,128]{1,0:T(8,128)(2,1)} %h_ref.1), custom_call_target="tpu_custom_call" | custom-call | tf_op jit(solution)/shard_map/pallas_call | solution.py:396
  105.0 0.0 copy-done
  105.0 4.0 %fusion = f32[4096,172]{0,1:T(8,128)} fusion(bf16[4096,256]{1,0:T(8,128)(2,1)} %shard_map.55, bf16[256,172]{0,1:T(8,128)(2,1)S(1)} %copy-done), kind=kOutput, calls=%fused_computation | convolution fusion | flops 360710144 | bytes 5003264 | tf_op jit(solution)/shard_map/dot_general | solution.py:430
Async XLA Ops:
  0.0 105.0 %copy-start = (bf16[256,172]{0,1:T(8,128)(2,1)S(1)}, bf16[256,172]{0,1:T(8,128)(2,1)}, u32[]{:S(2)}) copy-start(bf16[256,172]{0,1:T(8,128)(2,1)} %param.9) | copy-start | bytes 264196

commit v3 on v2

--- a/solution.py
+++ b/solution.py
@@ -28,9 +28,9 @@
 
 def kernel(mask_ref, w1_ref, a_ref, h_ref, y2_ref,
            abuf_r, abuf_c, hbuf, ht, w1t, pbuf_s, pbuf_r, mbuf_s, mbuf_r, own1, ybuf, ybuf_i, z, zt,
-           dfb, tms, tmr, acc2, tfb, y2s,
+           dfb, tms, tmr, acc2, tfb,
            ar_sem, ac_sem, h_sem, hx_s, hx_r, pf_s, pf_r, mf_s, mf_r, pb_s, pb_r, mb_s, mb_r, yb_s, yb_r,
-           df_s, df_r, tm_s, tm_r, tf_s, tf_r, ob_s, ob_r, out_sem):
+           df_s, df_r, tm_s, tm_r, tf_s, tf_r, ob_s, ob_r):
     rep = lax.axis_index('rep')
     row = lax.axis_index('rows')
     chip_x = row // 2
@@ -53,7 +53,7 @@
         return pltpu.make_async_copy(a_ref.at[:, pl.ds(pl.multiple_of(k * BLK + q * CH, CH), CH)], abuf_c.at[slot, k], ac_sem.at[slot, k])
 
     def h_send():
-        return remote(h_ref, hbuf.at[core], hx_s, hx_r, mate)
+        return remote(hbuf.at[core], hbuf.at[core], hx_s, hx_r, mate)
 
     def pf(r):
         return remote(pbuf_s.at[r], pbuf_r.at[r], pf_s.at[r], pf_r.at[r], partner)
@@ -88,10 +88,7 @@
         return y2_ref.at[pl.ds(pl.multiple_of(m * CH + p * PC, PC), PC), :]
 
     def ob(m, p):
-        return remote(y2s.at[m, pl.ds(p * PC, PC), :], out_rows(m, p), ob_s.at[m, p], ob_r.at[m, p], yside)
-
-    def out_copy(m, p):
-        return pltpu.make_async_copy(y2s.at[m, pl.ds(p * PC, PC), :], out_rows(m, p), out_sem.at[m, p])
+        return remote(out_rows(m, p), out_rows(m, p), ob_s.at[m, p], ob_r.at[m, p], yside)
 
     def mask_of(dst_blk, src_blk):
         return mask_ref[dst_blk, src_blk].astype(F32)
@@ -100,12 +97,9 @@
         hid = jnp.maximum(jnp.dot(ybuf[k, m], w1_ref[...], preferred_element_type=F32), 0.0)
         z[pl.ds(pl.multiple_of(k * BLK + m * CH, CH), CH), :] = (hid * mask_of(row, rep * 2 + k)).astype(BF16)
 
-    def barrier():
-        sem = pltpu.get_barrier_semaphore()
-        for dev in (partner, mate, yside):
-            pl.semaphore_signal(sem, inc=1, device_id=dev, device_id_type=MESH)
-        pl.semaphore_wait(sem, 3)
-
+    barrier = pltpu.get_barrier_semaphore()
+    for dev in (partner, mate, yside):
+        pl.semaphore_signal(barrier, inc=1, device_id=dev, device_id_type=MESH)
     h_own = pltpu.make_async_copy(h_ref, hbuf.at[core], h_sem)
     h_own.start()
 
@@ -122,7 +116,17 @@
                     col_copy(t, t, k).start()
 
     first_loads(0, 1)
-    barrier()
+    h_own.wait()
+    first_loads(1, 2)
+
+    @pl.when(jnp.logical_not(diag))
+    def _():
+        def turn(m):
+            piece = hbuf[core, pl.ds(pl.multiple_of(m * CH, CH), CH), :]
+            ht[:, pl.ds(pl.multiple_of(m * CH, CH), CH)] = piece.astype(F32).T.astype(BF16)
+        loop(0, NCH, turn)
+
+    pl.semaphore_wait(barrier, 3)
 
     @pl.when(diag)
     def _():
@@ -140,9 +144,6 @@
             def _():
                 row_copy(chunk_at(nxt), nxt % NBUF).start()
 
-        h_own.wait()
-        first_loads(1, NBUF)
-
         def product1_of(slot, k, dst):
             cols = pl.ds(pl.multiple_of(k * BLK, BLK), BLK)
             return jnp.dot(abuf_r[slot, :, cols], hbuf[k], preferred_element_type=F32) * mask_of(dst, rep * 2 + k)
@@ -154,7 +155,8 @@
 
         row_copy(0, 0).wait()
         pbuf_s[0] = product1_of(0, core, row)
-        remote(h_ref, hbuf.at[other], hx_s, hx_r, mate).wait_recv()
+        first_loads(2, NBUF)
+        remote(hbuf.at[other], hbuf.at[other], hx_s, hx_r, mate).wait_recv()
         pbuf_s[0] = pbuf_s[0] + product1_of(0, other, row)
         pf(0).start()
         next_load(0)
@@ -204,18 +206,18 @@
             half = s // 2
             for p in range(NPC):
                 rows = pl.ds(p * PC, PC)
+                dst = pl.ds(pl.multiple_of(m * CH + p * PC, PC), PC)
 
                 @pl.when(s % 2 == 0)
                 def _():
                     df(half, p).wait_recv()
-                    y2s[m, rows, :] = (acc2[s % 2, rows, :] + dfb[half, rows, :]).astype(BF16)
+                    y2_ref[dst, :] = (acc2[s % 2, rows, :] + dfb[half, rows, :]).astype(BF16)
 
                 @pl.when(s % 2 == 1)
                 def _():
                     tf(half, p).wait_recv()
-                    y2s[m, rows, :] = (acc2[s % 2, rows, :] + tfb[half, rows, :]).astype(BF16)
+                    y2_ref[dst, :] = (acc2[s % 2, rows, :] + tfb[half, rows, :]).astype(BF16)
                 ob(m, p).start()
-                out_copy(m, p).start()
 
         product2(0)
 
@@ -237,7 +239,6 @@
             mb_out(m).wait_send()
             for p in range(NPC):
                 ob(m, p).wait_send()
-                out_copy(m, p).wait()
         loop(0, NCH, drain)
 
     @pl.when(jnp.logical_not(diag))
@@ -254,13 +255,6 @@
         def cols_wait(slot):
             for k in range(2):
                 col_copy(0, slot, k).wait()
-
-        h_own.wait()
-
-        def turn(m):
-            piece = hbuf[core, pl.ds(pl.multiple_of(m * CH, CH), CH), :]
-            ht[:, pl.ds(pl.multiple_of(m * CH, CH), CH)] = piece.astype(F32).T.astype(BF16)
-        loop(0, NCH, turn)
 
         mask_own = mask_of(blk_own, row)
         mask_other = mask_of(blk_other, row)
@@ -293,14 +287,17 @@
             hidden_rows(core, m)
 
         produce1_other(0)
-        first_loads(1, NBUF)
+        first_loads(2, NBUF)
         produce1_own(0)
+        combine_send(0)
+        produce1_other(1)
+        produce1_own(1)
 
         def send_half(t):
             produce1_other(t + 1)
             combine_send(t)
             produce1_own(t + 1)
-        loop(0, HALF, send_half)
+        loop(1, HALF, send_half)
 
         def keep_half(r):
             produce1_other(r + HALF + 1)
@@ -395,9 +392,9 @@
         dma = pltpu.SemaphoreType.DMA
         y_two = pl.pallas_call(
             kernel,
-            out_shape=jax.ShapeDtypeStruct((BLK, F1), BF16),
+            out_shape=pltpu.VMEM((BLK, F1), BF16),
             in_specs=[pl.BlockSpec(memory_space=pltpu.SMEM), pl.BlockSpec(memory_space=pltpu.VMEM), pl.BlockSpec(memory_space=pl.ANY), pl.BlockSpec(memory_space=pl.ANY)],
-            out_specs=pl.BlockSpec(memory_space=pl.ANY),
+            out_specs=pl.BlockSpec(memory_space=pltpu.VMEM),
             scratch_shapes=[
                 pltpu.VMEM((NBUF, CH, 2 * BLK), BF16),
                 pltpu.VMEM((NBUF, 2, BLK, CH), BF16),
@@ -418,14 +415,13 @@
                 pltpu.VMEM((HALF, F1, CH), F32),
                 pltpu.VMEM((2, F1, CH), F32),
                 pltpu.VMEM((HALF, CH, F1), F32),
-                pltpu.VMEM((NCH, CH, F1), BF16),
                 dma((NBUF,)), dma((NBUF, 2)), dma, dma, dma,
                 dma((HALF,)), dma((HALF,)), dma((NCH,)), dma((NCH,)), dma((HALF,)), dma((HALF,)),
                 dma((NCH,)), dma((NCH,)), dma((NCH,)), dma((NCH,)),
                 dma((HALF, NPC)), dma((HALF, NPC)), dma((HALF,)), dma((HALF,)), dma((HALF, NPC)), dma((HALF, NPC)),
-                dma((NCH, NPC)), dma((NCH, NPC)), dma((NCH, NPC)),
+                dma((NCH, NPC)), dma((NCH, NPC)),
             ],
-            compiler_params=pltpu.CompilerParams(collective_id=0, has_side_effects=True, vmem_limit_bytes=66 * 1000 * 1000),
+            compiler_params=pltpu.CompilerParams(collective_id=0, has_side_effects=True, vmem_limit_bytes=56 * 2 ** 20),
         )(block_mask, w_one, adj_local, feat_blk)
         return jnp.dot(y_two, w_two, preferred_element_type=F32)
 

time: 109 us -> 106 us (0.972)
  matrix products: 4.01 us -> 2.42 us
    dot_general x1, matrix products: 4.01 us -> 2.42 us  [local_fn(): return jnp.dot(y_two, w_two, preferred_element_type=F32)]
    pallas_call x1, Pallas kernels: 105 us -> 104 us  [local_fn(): pl.pallas_call(kernel, out_shape=pltpu.VMEM((BLK, F1), BF16), in_specs=[p...]
where the time goes in v3:
time: 106 us
  Pallas kernels  104 us (98%)
  matrix products  2.42 us (2%)
    pallas_call x1, Pallas kernels, local_fn(): pl.pallas_call(kernel, out_shape=pltpu.VMEM((BLK, F1), BF16), in_specs=[p...  104 us
    dot_general x1, matrix products, local_fn(): return jnp.dot(y_two, w_two, preferred_element_type=F32)  2.42 us

profile of v3, /device:TPU:0, one launch (start us, length us, event | category | flops | bytes accessed | tf_op | source)
XLA Modules:
  0.0 106.2 jit_solution(1489813975742344344)
XLA Ops:
  0.0 0.0 copy-start
  0.0 103.8 %shard_map.55 = bf16[4096,256]{1,0:T(8,128)(2,1)S(1)} custom-call(s32[4,4]{1,0:T(4,128)} %mask_ref.1, bf16[128,256]{1,0:T(8,128)(2,1)} %w1_ref.1, bf16[4096,8192]{1,0:T(8,128)(2,1)} %a_ref.1, bf16[4096,128]{1,0:T(8,128)(2,1)} %h_ref.1), custom_call_target="tpu_custom_call" | custom-call | tf_op jit(solution)/shard_map/pallas_call | solution.py:393
  103.8 0.0 copy-done
  103.8 2.4 %fusion = f32[4096,172]{0,1:T(8,128)} fusion(bf16[4096,256]{1,0:T(8,128)(2,1)S(1)} %shard_map.55, bf16[256,172]{0,1:T(8,128)(2,1)S(1)} %copy-done), kind=kOutput, calls=%fused_computation | convolution fusion | flops 360710144 | bytes 5003264 | tf_op jit(solution)/shard_map/dot_general | solution.py:426
Async XLA Ops:
  0.0 103.8 %copy-start = (bf16[256,172]{0,1:T(8,128)(2,1)S(1)}, bf16[256,172]{0,1:T(8,128)(2,1)}, u32[]{:S(2)}) copy-start(bf16[256,172]{0,1:T(8,128)(2,1)} %param.9) | copy-start | bytes 264196

commit v4 on v3

--- a/solution.py
+++ b/solution.py
@@ -43,6 +43,8 @@
     blk_own = rep * 2 + core
     blk_other = rep * 2 + other
 
+    block = pl.when(row + rep < 64)
+
     def remote(src, dst, send, recv, dev):
         return pltpu.make_async_remote_copy(src_ref=src, dst_ref=dst, send_sem=send, recv_sem=recv, device_id=dev, device_id_type=MESH)
 
@@ -162,31 +164,40 @@
         next_load(0)
 
         def send_half(t):
-            pbuf_s[t] = product1(t)
-            pf(t).start()
+            @block
+            def _():
+                pbuf_s[t] = product1(t)
+                pf(t).start()
             next_load(t)
         loop(1, HALF, send_half)
 
         def keep_half(r):
             t = r + HALF
-            part = product1(t)
+            @block
+            def _():
+                part = product1(t)
+                pf(r).wait_recv()
+                ybuf[core, r] = (part + pbuf_r[r]).astype(BF16)
+                pb(r, r).start()
+                yb(r).start()
+                mb_out(r).start()
             next_load(t)
-            pf(r).wait_recv()
-            ybuf[core, r] = (part + pbuf_r[r]).astype(BF16)
-            pb(r, r).start()
-            yb(r).start()
-            mb_out(r).start()
             hidden_rows(core, r)
         loop(0, HALF, keep_half)
 
         def relay(r):
             m = r + HALF
-            pb(m, r).wait_recv()
-            yb(m).start()
-            mb_out(m).start()
-            hidden_rows(core, m)
-            mb_in(r).wait_recv()
-            hidden_rows(other, r)
+            @block
+            def _():
+                pb(m, r).wait_recv()
+                yb(m).start()
+                mb_out(m).start()
+
+            @block
+            def _():
+                hidden_rows(core, m)
+                mb_in(r).wait_recv()
+                hidden_rows(other, r)
         loop(0, HALF, relay)
 
         def rest(r):
@@ -262,11 +273,16 @@
         def produce1_other(t):
             slot = t % NBUF
             cols_wait(slot)
-            mbuf_s[t] = jnp.dot(ht[...], abuf_c[slot, other], preferred_element_type=F32) * mask_other
-            mf(t).start()
+
+            @block
+            def _():
+                mbuf_s[t] = jnp.dot(ht[...], abuf_c[slot, other], preferred_element_type=F32) * mask_other
+                mf(t).start()
 
         def produce1_own(t):
-            own1[t % 2] = jnp.dot(ht[...], abuf_c[t % NBUF, core], preferred_element_type=F32) * mask_own
+            @block
+            def _():
+                own1[t % 2] = jnp.dot(ht[...], abuf_c[t % NBUF, core], preferred_element_type=F32) * mask_own
             next_cols(t)
 
         def combine1(t):
@@ -274,17 +290,25 @@
             return (own1[t % 2] + mbuf_r[t]).T
 
         def combine_send(t):
-            pbuf_s[t] = combine1(t)
-            pf(t).start()
+            @block
+            def _():
+                pbuf_s[t] = combine1(t)
+                pf(t).start()
 
         def combine_keep(r):
             m = r + HALF
-            part = combine1(m)
-            pf(r).wait_recv()
-            ybuf[core, m] = (part + pbuf_r[r]).astype(BF16)
-            pb(m, r).start()
-            mb_out(m).start()
-            hidden_rows(core, m)
+
+            @block
+            def _():
+                part = combine1(m)
+                pf(r).wait_recv()
+                ybuf[core, m] = (part + pbuf_r[r]).astype(BF16)
+                pb(m, r).start()
+                mb_out(m).start()
+
+            @block
+            def _():
+                hidden_rows(core, m)
 
         produce1_other(0)
         first_loads(2, NBUF)
@@ -316,8 +340,10 @@
             zt[:, pl.ds(pl.multiple_of(m * CH, CH), CH)] = jnp.maximum(hid, 0.0).astype(BF16)
 
         def relay(r):
-            pb(r, r).wait_recv()
-            mb_out(r).start()
+            @block
+            def _():
+                pb(r, r).wait_recv()
+                mb_out(r).start()
             hidden_rows(core, r)
             mb_in(r + HALF).wait_recv()
             hidden_rows(other, r + HALF)
@@ -332,9 +358,12 @@
         def direct(m):
             slot = m % NBUF
             row_copy(0, slot).wait()
-            dfb[m] = jnp.dot(abuf_r[slot], z[...], preferred_element_type=F32)
-            for p in range(NPC):
-                df(m, p).start()
+
+            @block
+            def _():
+                dfb[m] = jnp.dot(abuf_r[slot], z[...], preferred_element_type=F32)
+                for p in range(NPC):
+                    df(m, p).start()
 
             @pl.when(m + NBUF < HALF)
             def _():
@@ -343,18 +372,26 @@
         def turned_other(m):
             slot = (m + NCH) % NBUF
             cols_wait(slot)
-            tms[m] = jnp.dot(zt[...], abuf_c[slot, other], preferred_element_type=F32) * mask_other
-            tm(m).start()
+
+            @block
+            def _():
+                tms[m] = jnp.dot(zt[...], abuf_c[slot, other], preferred_element_type=F32) * mask_other
+                tm(m).start()
 
         def turned_own(m):
             t = m + NCH
-            own = jnp.dot(zt[...], abuf_c[t % NBUF, core], preferred_element_type=F32) * mask_own
+
+            @block
+            def _():
+                acc2[0] = jnp.dot(zt[...], abuf_c[t % NBUF, core], preferred_element_type=F32) * mask_own
             next_cols(t)
-            acc2[0] = own
-            tm(m).wait_recv()
-            tfb[m] = (acc2[0] + tmr[m]).T
-            for p in range(NPC):
-                tf(m, p).start()
+
+            @block
+            def _():
+                tm(m).wait_recv()
+                tfb[m] = (acc2[0] + tmr[m]).T
+                for p in range(NPC):
+                    tf(m, p).start()
 
         direct(0)
         loop(HALF, NCH, hidden_turned)

time: 106 us -> 105 us (level)
  Pallas kernels: 104 us -> 102 us
    pallas_call x1, Pallas kernels: 104 us -> 102 us  [local_fn(): pl.pallas_call(kernel, out_shape=pltpu.VMEM((BLK, F1), BF16), in_specs=[p...]
where the time goes in v4:
time: 105 us
  Pallas kernels  102 us (97%)
  matrix products  2.42 us (2%)
    pallas_call x1, Pallas kernels, local_fn(): pl.pallas_call(kernel, out_shape=pltpu.VMEM((BLK, F1), BF16), in_specs=[p...  102 us
    dot_general x1, matrix products, local_fn(): return jnp.dot(y_two, w_two, preferred_element_type=F32)  2.42 us

profile of v4, /device:TPU:0, one launch (start us, length us, event | category | flops | bytes accessed | tf_op | source)
XLA Modules:
  0.0 104.8 jit_solution(3333645903297603141)
XLA Ops:
  0.0 0.0 copy-start
  0.0 102.4 %shard_map.55 = bf16[4096,256]{1,0:T(8,128)(2,1)S(1)} custom-call(s32[4,4]{1,0:T(4,128)} %mask_ref.1, bf16[128,256]{1,0:T(8,128)(2,1)} %w1_ref.1, bf16[4096,8192]{1,0:T(8,128)(2,1)} %a_ref.1, bf16[4096,128]{1,0:T(8,128)(2,1)} %h_ref.1), custom_call_target="tpu_custom_call" | custom-call | tf_op jit(solution)/shard_map/pallas_call | solution.py:430
  102.4 0.0 copy-done
  102.4 2.4 %fusion = f32[4096,172]{0,1:T(8,128)} fusion(bf16[4096,256]{1,0:T(8,128)(2,1)S(1)} %shard_map.55, bf16[256,172]{0,1:T(8,128)(2,1)S(1)} %copy-done), kind=kOutput, calls=%fused_computation | convolution fusion | flops 360710144 | bytes 5003264 | tf_op jit(solution)/shard_map/dot_general | solution.py:463
Async XLA Ops:
  0.0 102.4 %copy-start = (bf16[256,172]{0,1:T(8,128)(2,1)S(1)}, bf16[256,172]{0,1:T(8,128)(2,1)}, u32[]{:S(2)}) copy-start(bf16[256,172]{0,1:T(8,128)(2,1)} %param.9) | copy-start | bytes 264196
